TPU v7x, 512 devices: a 8x2x16 block of a 8x8x16 slice. The times are simulated.
512 devices in a mesh: groups: 2 (over y), seq: 16 (over z), heads: 8 (over x), sub: 2 (over core).
Axes of the slice: x: 8, y: 2, z: 16, core: 2. Of those that a mesh axis runs over, the one named last changes fastest.
The devices are a block of a 8x8x16 slice.
Arguments:
- queries: bfloat16 [8192, 8192], P(('groups', 'seq', 'sub'), 'heads'), parts along dimension 0, may hold values from -400 to 400
- keys: bfloat16 [8192, 1024], P(('groups', 'seq', 'sub'), 'heads'), parts along dimension 0, may hold values from -6 to 6
- values: bfloat16 [8192, 1024], P(('groups', 'seq', 'sub'), 'heads'), parts along dimension 0, may hold values from -18 to 18
- half_order: int32 [128], P('groups'), parts along dimension 0, may hold values from 0 to 63, as said below
- frame_lengths: int32 [64], P('groups'), parts along dimension 0, may hold values from 1 to 256, 4096 in all
- out_proj: bfloat16 [8192, 4096], P('heads', ('seq', 'sub')), may hold values from -0.125 to 0.125
- residual_in: bfloat16 [8192, 4096], P(('groups', 'seq', 'sub'), 'heads'), parts along dimension 0, may hold values from -40 to 40
- norm_gain: float32 [4096], P('heads'), may hold values from 0.5 to 1.5
Outputs:
- attended: bfloat16 [8192, 8192], P(('groups', 'seq', 'sub'), 'heads'), parts along dimension 0
- hidden_state: bfloat16 [8192, 4096], P(('groups', 'seq', 'sub'), 'heads'), parts along dimension 0
- normed: bfloat16 [8192, 4096], P(('groups', 'seq', 'sub'), 'heads'), parts along dimension 0
There are 2 independent parts, one for each index of `groups`. A program takes and returns all parts, laid end to end along the dimension named above; an argument that names none is the same for every part. Nothing has to cross between parts.
Inputs may be any that keep to these rules, and one draw needn't show every extreme that they name: `half_order`: a permutation of 0 to 63.
All inputs are finite; a program needn't handle non-finite values.
Results may differ from a plain program's by a relative error of at most 0.005.
Values may be sent and summed in bfloat16 or wider, within the bound.
A program may use at most 64 MiB of HBM per device.

v0:
```python
import jax
import jax.numpy as jnp
from jax import lax
from jax.sharding import PartitionSpec as P

HEAD_WIDTH = 128
OUT_WIDTH = 4096


def side_by_side(arrays, axis, dim, along):
    ends, at = ([], 0)
    for a in arrays[:-1]:
        at += a.shape[along]
        ends.append(at)
    both = jnp.concatenate(arrays, axis=along)
    return tuple(jnp.split(lax.all_gather(both, axis, axis=dim, tiled=True), ends, axis=along))


def split_up(value, dim, devices):
    shape = value.shape
    parts = value.reshape(*shape[:dim], devices, shape[dim] // devices, *shape[dim + 1 :])
    return jnp.moveaxis(parts, dim, 0)


def summed_on_arrival(value, axis, dim):
    devices = lax.axis_size(axis)
    parts = lax.all_to_all(split_up(value, dim, devices), axis, 0, 0, tiled=True)
    return jnp.sum(parts.astype(jnp.float32), axis=0)


def from_everyone(value, axis):
    copies = jnp.broadcast_to(value, (lax.axis_size(axis), *value.shape))
    return lax.all_to_all(copies, axis, split_axis=0, concat_axis=0, tiled=True)


def of_everyone(value, axis):
    return from_everyone(value, axis).sum(axis=0)


def shards(queries, keys, values, half_order, frame_lengths, out_proj, residual_in, norm_gain):
    tok_rows = queries.shape[0]
    kv_local = keys.shape[1] // HEAD_WIDTH
    group_width = queries.shape[1] // keys.shape[1]
    half_rows = tok_rows // 2
    own_index = lax.axis_index("seq") * lax.axis_size("sub") + lax.axis_index("sub")
    table_ids = jnp.arange(half_order.shape[0], dtype=jnp.int32)

    def locate(row_ids):
        matches = (row_ids // half_rows)[:, None] == table_ids[None, :]
        offsets = jnp.sum(jnp.where(matches, half_order[None, :], 0), axis=1)
        return offsets * half_rows + row_ids % half_rows

    query_pos = locate(own_index * tok_rows + jnp.arange(tok_rows, dtype=jnp.int32))
    frame_ends = jnp.cumsum(frame_lengths)
    frame_starts = frame_ends - frame_lengths
    frame_limit = jnp.sum(
        jnp.where(frame_starts[None, :] <= query_pos[:, None], frame_lengths[None, :], 0), axis=1
    )
    query_head_rows = queries.reshape(tok_rows, kv_local, group_width, HEAD_WIDTH)
    score_scale = HEAD_WIDTH ** (-0.5)
    initial = (
        jnp.full((kv_local, group_width, tok_rows), -1e30, jnp.float32),
        jnp.zeros((kv_local, group_width, tok_rows), jnp.float32),
        jnp.zeros((kv_local, group_width, tok_rows, HEAD_WIDTH), jnp.float32),
    )
    key_piece, value_piece = side_by_side((keys, values), ("seq", "sub"), 0, 1)
    piece_rows = key_piece.shape[0]
    key_pos = locate(jnp.arange(piece_rows, dtype=jnp.int32))

    def absorb_piece(current):
        running_max, denominator, numerator = current
        key_view = key_piece.reshape(piece_rows, kv_local, HEAD_WIDTH)
        value_view = value_piece.reshape(piece_rows, kv_local, HEAD_WIDTH)
        scores = (
            jnp.einsum(
                "qhgd,khd->hgqk", query_head_rows, key_view, preferred_element_type=jnp.float32
            )
            * score_scale
        )
        visible = key_pos[None, :] < frame_limit[:, None]
        scores = jnp.where(visible, scores, -1e30)
        new_max = jnp.maximum(running_max, jnp.max(scores, axis=-1))
        weights = jnp.where(visible, jnp.exp(scores - new_max[..., None]), 0.0)
        denominator = jnp.sum(weights, axis=-1)
        product = jnp.einsum(
            "hgqk,khd->hgqd",
            weights.astype(jnp.bfloat16),
            value_view,
            preferred_element_type=jnp.float32,
        )
        numerator = product
        return (new_max, denominator, numerator)

    running_max, denominator, numerator = lax.cond(
        jnp.min(key_pos) < jnp.max(frame_limit), absorb_piece, lambda current: current, initial
    )
    result = numerator / denominator[..., None]
    attended = (
        jnp.transpose(result, (2, 0, 1, 3))
        .reshape(tok_rows, kv_local * group_width * HEAD_WIDTH)
        .astype(jnp.bfloat16)
    )
    head_terms = jnp.dot(
        attended,
        lax.all_gather(out_proj, ("seq", "sub"), axis=1, tiled=True),
        preferred_element_type=jnp.float32,
    )
    projected = summed_on_arrival(head_terms.astype(jnp.bfloat16), "heads", 1)
    hidden_state = (residual_in.astype(jnp.float32) + projected).astype(jnp.bfloat16)
    widened = hidden_state.astype(jnp.float32)
    energy = of_everyone(jnp.sum(widened * widened, axis=1), "heads") / OUT_WIDTH
    normed = (widened * lax.rsqrt(energy + 1e-06)[:, None] * norm_gain[None, :]).astype(
        jnp.bfloat16
    )
    return (attended, hidden_state, normed)


def solution(mesh):
    in_specs = (
        P(("groups", "seq", "sub"), "heads"),
        P(("groups", "seq", "sub"), "heads"),
        P(("groups", "seq", "sub"), "heads"),
        P("groups"),
        P("groups"),
        P("heads", ("seq", "sub")),
        P(("groups", "seq", "sub"), "heads"),
        P("heads"),
    )
    out_specs = (
        P(("groups", "seq", "sub"), "heads"),
        P(("groups", "seq", "sub"), "heads"),
        P(("groups", "seq", "sub"), "heads"),
    )
    return jax.shard_map(shards, mesh=mesh, in_specs=in_specs, out_specs=out_specs, check_vma=False)
```

profile of v0, /device:TPU:65, one launch (start us, length us, event | category | flops | bytes accessed | tf_op | source)
XLA Modules:
  0.0 272.1 jit_solution(6806642003269453513)
XLA Ops:
  7.2 0.1 all-gather.3.cloned.1.call-start
  7.2 1.4 pad_maximum_fusion
  8.7 0.1 all-gather.3.cloned.1.call-update
  8.7 0.1 all-gather.5.cloned.1.call-start
  8.8 0.7 all-gather.5.cloned.1.call-update
  9.5 0.7 copy.32
  10.3 0.1 reduce-window.9
  10.3 0.1 reduce.3
  10.5 0.7 sub.24
  11.1 0.7 select_reduce_fusion.1
  11.9 0.7 select_reduce_fusion.2
  12.6 0.6 reduce_max.18
  13.3 0.9 select_reduce_fusion
  14.2 0.6 fusion.33
  16.1 103.1 %all-gather.3.cloned.1.call-done = bf16[4096,256]{1,0:T(8,128)(2,1)} async-done(((bf16[128,256]{1,0:T(8,128)(2,1)}), bf16[4096,256]{1,0:T(8,128)(2,1)}) %all-gather.3.cloned.1.call-update) | async-done | bytes 2097168 | tf_op jit(solution)/shard_map/all_gather | solution.py:16
  119.3 14.2 %conditional.1 = (f32[1,8,128]{2,1,0:T(8,128)S(1)}, f32[1,8,128,128]{3,2,1,0:T(8,128)S(1)}) conditional(s32[]{:T(128)} %convert_element_type.33, () %tuple.16, (s32[4096]{0:T(1024)S(1)}, s32[128]{0:T(128)S(1)}, bf16[4096,256]{1,0:T(8,128)(2,1)}, bf16[128,1024]{1,0:T(8,128)(2,1)}) %tuple.17), branch_computations={%region_6.7_spmd, %region_7.10_spmd} | conditional | flops 2202532864 | bytes 63742508 | solution.py:94
  119.3 0.0 copy-start.4
  119.3 1.8 broadcast_compare_fusion
  121.1 3.8 %fusion = (f32[8,128]{1,0:T(8,128)S(1)}, f32[4096,128,8]{1,0,2:T(8,128)S(1)}) fusion(pred[128,4096]{0,1:T(8,128)(4,1)S(1)} %broadcast_compare_fusion, bf16[4096,256]{1,0:T(8,128)(2,1)} %get-tuple-element.14, bf16[128,1024]{1,0:T(8,128)(2,1)} %get-tuple-element.24), kind=kOutput, calls=%fused_computation.2 | convolution fusion | flops 1086323712 | bytes 18616320 | tf_op jit(solution)/shard_map/cond/branch_1_fun/qhgd,khd->hgqk/dot_general | solution.py:75
  124.9 0.0 copy-done.4
  124.9 4.4 %fusion.7 = f32[1,8,128,128]{3,2,1,0:T(8,128)S(1)} fusion(f32[4096,128,8]{1,0,2:T(8,128)S(1)} %get-tuple-element.30, f32[8,128]{1,0:T(8,128)S(1)} %broadcast_maximum_fusion, pred[128,4096]{0,1:T(8,128)(4,1)S(1)} %broadcast_compare_fusion, bf16[4096,256]{1,0:T(8,128)(2,1)S(1)} %copy-done.4), kind=kOutput, calls=%fused_computation.8 | convolution fusion | flops 1094713344 | bytes 18878464 | tf_op jit(solution)/shard_map/cond/branch_1_fun/hgqk,khd->hgqd/dot_general | solution.py:85
  129.4 4.0 %fusion.2 = f32[8,128]{1,0:T(8,128)S(1)} fusion(f32[4096,128,8]{1,0,2:T(8,128)S(1)} %get-tuple-element.30, f32[8,128]{1,0:T(8,128)S(1)} %broadcast_maximum_fusion, pred[128,4096]{0,1:T(8,128)(4,1)S(1)} %broadcast_compare_fusion), kind=kLoop, calls=%fused_computation.4 | loop fusion | flops 20970496 | bytes 17309696 | tf_op jit(solution)/shard_map/cond/branch_1_fun/reduce_sum | solution.py:84
  133.4 0.0 copy-start.2
  133.4 0.0 copy-start.3
  133.4 0.2 fusion.23
  133.7 0.2 copy.33
  133.9 0.0 copy-start
  133.9 81.7 %all-gather.5.cloned.1.call-done = bf16[1024,4096]{1,0:T(8,128)(2,1)} async-done(((bf16[1024,128]{1,0:T(8,128)(2,1)}), bf16[1024,4096]{1,0:T(8,128)(2,1)}) %all-gather.5.cloned.1.call-update) | async-done | bytes 8388624 | tf_op jit(solution)/shard_map/all_gather | solution.py:105
  215.6 4.6 %convolution_convert_fusion = bf16[128,4096]{1,0:T(8,128)(2,1)S(1)} fusion(bf16[128,1024]{1,0:T(8,128)(2,1)S(1)} %bitcast.64, bf16[1024,4096]{1,0:T(8,128)(2,1)} %all-gather.5.cloned.1.call-done), kind=kOutput, calls=%fused_computation.21 | convolution fusion | flops 1074266112 | bytes 9699328 | tf_op jit(solution)/shard_map/dot_general | solution.py:103
  220.3 0.1 copy.48
  220.3 34.8 %all_to_all.11 = bf16[8,128,512]{2,1,0:T(8,128)(2,1)S(1)} all-to-all(bf16[8,128,512]{2,1,0:T(8,128)(2,1)S(1)} %bitcast.62), channel_id=1, replica_groups=mesh['groups'=2,'seq'=16,'heads'=8,'sub'=2] {'heads'}, dimensions={0} | all-to-all | bytes 2097152 | tf_op jit(solution)/shard_map/all_to_all | solution.py:27
  255.2 0.1 convert_reduce_fusion
  255.3 0.0 copy-done.2
  255.3 0.1 fusion.20
  255.4 0.0 copy-start.1
  255.5 9.0 %all_to_all.12 = f32[8,1,128]{2,1,0:T(1,128)S(1)} all-to-all(f32[8,1,128]{2,1,0:T(1,128)S(1)} %broadcast_in_dim.81), channel_id=1, replica_groups=mesh['groups'=2,'seq'=16,'heads'=8,'sub'=2] {'heads'}, dimensions={0} | all-to-all | bytes 8192 | tf_op jit(solution)/shard_map/all_to_all | solution.py:33
  264.4 0.0 copy-done.3
  264.5 0.8 fusion.22
  265.2 0.0 copy-done
  265.2 0.0 copy-done.1
  (8 shorter events, 0.1 us)
Async XLA Ops:
  7.2 112.1 %all-gather.3.cloned.1.call-start = ((), (), s32[]{:S(2)}) async-start(), calls=%async_computation.2 | async-start | bytes 2162688 | tf_op jit(solution)/shard_map/all_gather | solution.py:16
  8.7 206.9 %all-gather.5.cloned.1.call-start = ((), (), s32[]{:S(2)}) async-start(), calls=%async_computation.3 | async-start | bytes 8650752 | tf_op jit(solution)/shard_map/all_gather | solution.py:105
  119.3 5.7 %copy-start.4 = (bf16[4096,256]{1,0:T(8,128)(2,1)S(1)}, bf16[4096,256]{1,0:T(8,128)(2,1)}, u32[]{:S(2)}) copy-start(bf16[4096,256]{1,0:T(8,128)(2,1)} %get-tuple-element.14) | copy-start | bytes 6291460 | tf_op jit(solution)/shard_map/cond
  133.4 121.9 %copy-start.2 = (bf16[128,512]{1,0:T(8,128)(2,1)S(1)}, bf16[128,512]{1,0:T(8,128)(2,1)}, u32[]{:S(2)}) copy-start(bf16[128,512]{1,0:T(8,128)(2,1)} %param.16) | copy-start | bytes 393220
  133.4 131.0 %copy-start.3 = (f32[512]{0:T(512)S(1)}, f32[512]{0:T(512)}, u32[]{:S(2)}) copy-start(f32[512]{0:T(512)} %param.17) | copy-start | bytes 6148
  133.9 131.3 %copy-start = (bf16[16,8,8,128]{3,1,2,0:T(8,128)(2,1)}, bf16[16,8,8,128]{3,1,2,0:T(8,128)(2,1)S(1)}, u32[]{:S(2)}) copy-start(bf16[16,8,8,128]{3,1,2,0:T(8,128)(2,1)S(1)} %copy.49) | copy-start | bytes 786436
  255.4 9.8 %copy-start.1 = (bf16[128,512]{1,0:T(8,128)(2,1)}, bf16[128,512]{1,0:T(8,128)(2,1)S(1)}, u32[]{:S(2)}) copy-start(bf16[128,512]{1,0:T(8,128)(2,1)S(1)} %get-tuple-element.26) | copy-start | bytes 393220
Sparse Core Ops, SparseCore 0:
  10.7 108.4 all-gather.2
  121.3 94.2 all-gather.4
where the time goes:
time: 272 us
  waiting for transfers between devices  186 us (68%)
  blocking collectives  43.8 us (16%)
  between operations  15.5 us (6%)
  other arithmetic  13.1 us (5%)
  matrix products  12.9 us (5%)
    all_gather x1, waiting for transfers between devices, side_by_side(): lax.all_gather(both, axis, axis=dim, tiled=True)  103 us
    all_gather x1, waiting for transfers between devices, shards(): lax.all_gather(out_proj, ('seq', 'sub'), axis=1, tiled=True)  81.7 us
    all_to_all x1, blocking collectives, summed_on_arrival(): lax.all_to_all(split_up(value, dim, devices), axis, 0, 0, tiled=True)  34.8 us
    all_to_all x1, blocking collectives, from_everyone(): return lax.all_to_all(copies, axis, split_axis=0, concat_axis=0, tiled=True)  8.97 us
  transfers between devices with their start and end apart: 2, of which 2 were waited for; matrix products, arithmetic and copies ran while one was open for 7% of the time, Pallas kernels for 0%

commit v1 on v0

--- a/solution.py
+++ b/solution.py
@@ -5,6 +5,11 @@
 
 HEAD_WIDTH = 128
 OUT_WIDTH = 4096
+
+
+def gather_by_exchange(x, axis, dim):
+    copies = jnp.concatenate([x] * lax.axis_size(axis), axis=dim)
+    return lax.all_to_all(copies, axis, dim, dim, tiled=True)
 
 
 def side_by_side(arrays, axis, dim, along):
@@ -102,7 +107,7 @@
     )
     head_terms = jnp.dot(
         attended,
-        lax.all_gather(out_proj, ("seq", "sub"), axis=1, tiled=True),
+        gather_by_exchange(out_proj, ("seq", "sub"), 1),
         preferred_element_type=jnp.float32,
     )
     projected = summed_on_arrival(head_terms.astype(jnp.bfloat16), "heads", 1)

time: 272 us -> 518 us (1.90); the launches traced: 272 us -> 510 us
  waiting for transfers between devices: 186 us -> 352 us
  starting transfers between devices: 0.13 us -> 46.4 us
  local copies, waits for them, and re-layouts: 1.07 us -> 29.1 us
    all_to_all x0 -> x1, waiting for transfers between devices: none -> 242 us  [gather_by_exchange(): return lax.all_to_all(copies, axis, dim, dim, tiled=True)]
    all_gather x1 -> x0, waiting for transfers between devices: 81.7 us -> none  [shards(): lax.all_gather(out_proj, ('seq', 'sub'), axis=1, tiled=True)]
    all_to_all x0 -> x1, starting transfers between devices: none -> 46.3 us  [gather_by_exchange(): return lax.all_to_all(copies, axis, dim, dim, tiled=True)]
    all_to_all x0 -> x2, local copies, waits for them, and re-layouts: none -> 23.7 us  [gather_by_exchange(): return lax.all_to_all(copies, axis, dim, dim, tiled=True)]
    all_gather x1, waiting for transfers between devices: 103 us -> 110 us  [side_by_side(): lax.all_gather(both, axis, axis=dim, tiled=True)]
  transfers between devices with their start and end apart: 2 -> 2, of which waited for: 2 -> 2; matrix products, arithmetic and copies ran while one was open for 7% -> 3% of each run, Pallas kernels for 0% -> 0%
where the time goes in v1:
time: 518 us; the launch traced here: 510 us
  waiting for transfers between devices  352 us (68%)
  starting transfers between devices  46.4 us (9%)
  blocking collectives  42.7 us (8%)
  local copies, waits for them, and re-layouts  29.1 us (6%)
  between operations  15.8 us (3%)
  matrix products  14.7 us (3%)
  other arithmetic  9.67 us (2%)
    all_to_all x1, waiting for transfers between devices, gather_by_exchange(): return lax.all_to_all(copies, axis, dim, dim, tiled=True)  242 us
    all_gather x1, waiting for transfers between devices, side_by_side(): lax.all_gather(both, axis, axis=dim, tiled=True)  110 us
    all_to_all x1, starting transfers between devices, gather_by_exchange(): return lax.all_to_all(copies, axis, dim, dim, tiled=True)  46.3 us
    all_to_all x1, blocking collectives, summed_on_arrival(): lax.all_to_all(split_up(value, dim, devices), axis, 0, 0, tiled=True)  33.7 us
    all_to_all x2, local copies, waits for them, and re-layouts, gather_by_exchange(): return lax.all_to_all(copies, axis, dim, dim, tiled=True)  23.7 us
  transfers between devices with their start and end apart: 2, of which 2 were waited for; matrix products, arithmetic and copies ran while one was open for 3% of the time, Pallas kernels for 0%

profile of v1, /device:TPU:65, one launch (start us, length us, event | category | flops | bytes accessed | tf_op | source)
XLA Modules:
  0.0 510.1 jit_solution(1944826420030375603)
XLA Ops:
  7.2 1.1 copy.107
  9.1 0.0 copy-start
  9.2 3.2 copy-done
  12.4 11.9 %copy.139 = bf16[1024,32,128]{2,0,1:T(8,128)(2,1)} copy(bf16[1024,32,128]{0,2,1:T(8,128)(2,1)} %bitcast.65) | data formatting | bytes 16777216 | tf_op jit(solution)/shard_map/all_to_all | solution.py:12
  24.2 0.0 copy-start.4
  24.2 0.0 copy-start.5
  24.2 0.0 copy-start.10
  24.3 46.3 %all-to-all-start = ((bf16[1024,32,128]{2,0,1:T(8,128)(2,1)}), bf16[1024,32,128]{2,0,1:T(8,128)(2,1)}, u32[]{:S(2)}, u32[]{:S(2)}) async-start(bf16[1024,32,128]{2,0,1:T(8,128)(2,1)} %copy.139), calls=%async_computation | async-start | bytes 16777216 | tf_op jit(solution)/shard_map/all_to_all | solution.py:12
  70.6 0.1 all-gather.2.cloned.1.call-start
  70.6 0.0 copy-done.4
  70.6 0.0 copy-done.5
  70.7 0.6 pad_maximum_fusion
  71.3 0.1 all-gather.2.cloned.1.call-update
  71.4 0.0 copy-done.7
  71.4 0.1 copy.105
  71.5 0.1 reduce-window.9
  71.5 0.1 reduce.3
  71.7 0.0 copy-done.8
  71.7 0.1 select_reduce_fusion.1
  71.8 0.1 select_reduce_fusion.2
  71.9 0.6 reduce_max.18
  72.5 0.2 select_reduce_fusion
  72.8 0.6 fusion.33
  74.7 109.7 %all-gather.2.cloned.1.call-done = bf16[4096,256]{1,0:T(8,128)(2,1)} async-done(((bf16[128,256]{1,0:T(8,128)(2,1)}), bf16[4096,256]{1,0:T(8,128)(2,1)}) %all-gather.2.cloned.1.call-update) | async-done | bytes 2097168 | tf_op jit(solution)/shard_map/all_gather | solution.py:21
  184.4 0.0 copy-done.10
  184.4 14.5 %conditional.1 = (f32[1,8,128]{2,1,0:T(8,128)S(1)}, f32[1,8,128,128]{3,2,1,0:T(8,128)S(1)}) conditional(s32[]{:T(128)} %convert_element_type.35, () %tuple.16, (s32[4096]{0:T(1024)S(1)}, s32[128]{0:T(128)S(1)}, bf16[4096,256]{1,0:T(8,128)(2,1)}, bf16[128,1024]{1,0:T(8,128)(2,1)S(1)}) %tuple.26), branch_computations={%region_6.7_spmd, %region_7.10_spmd} | conditional | flops 2202532864 | bytes 63742508 | solution.py:99
  184.4 1.8 broadcast_compare_fusion
  186.2 0.0 copy-start.9
  186.2 3.9 fusion
  190.2 0.0 copy-done.9
  190.2 4.4 fusion.7
  194.7 4.0 fusion.2
  198.9 0.2 fusion.23
  199.1 0.2 copy.106
  199.3 0.0 copy-start.1
  199.3 241.9 %all-to-all-done = bf16[1024,32,128]{2,0,1:T(8,128)(2,1)} async-done(((bf16[1024,32,128]{2,0,1:T(8,128)(2,1)}), bf16[1024,32,128]{2,0,1:T(8,128)(2,1)}, u32[]{:S(2)}, u32[]{:S(2)}) %all-to-all-start) | async-done | bytes 8388640 | tf_op jit(solution)/shard_map/all_to_all | solution.py:12
  441.2 11.9 %copy.140 = bf16[1024,32,128]{0,2,1:T(8,128)(2,1)} copy(bf16[1024,32,128]{2,0,1:T(8,128)(2,1)} %all-to-all-done) | data formatting | bytes 16777216 | tf_op jit(solution)/shard_map/all_to_all | solution.py:12
  453.1 0.0 copy-done.1
  453.1 6.3 %convolution_convert_fusion = bf16[128,4096]{1,0:T(8,128)(2,1)S(1)} fusion(bf16[128,1024]{1,0:T(8,128)(2,1)S(1)} %bitcast.68, bf16[1024,4096]{0,1:T(8,128)(2,1)} %bitcast.64), kind=kOutput, calls=%fused_computation.21 | convolution fusion | flops 1074266112 | bytes 9699328 | tf_op jit(solution)/shard_map/dot_general | solution.py:108
  459.4 0.1 copy.155
  459.5 33.7 %all_to_all.23 = bf16[8,128,512]{2,1,0:T(8,128)(2,1)S(1)} all-to-all(bf16[8,128,512]{2,1,0:T(8,128)(2,1)S(1)} %bitcast.67), channel_id=1, replica_groups=mesh['groups'=2,'seq'=16,'heads'=8,'sub'=2] {'heads'}, dimensions={0} | all-to-all | bytes 2097152 | tf_op jit(solution)/shard_map/all_to_all | solution.py:32
  493.2 0.1 convert_reduce_fusion
  493.3 0.0 copy-done.3
  493.3 0.1 fusion.20
  493.4 9.0 %all_to_all.24 = f32[8,1,128]{2,1,0:T(1,128)S(1)} all-to-all(f32[8,1,128]{2,1,0:T(1,128)S(1)} %broadcast_in_dim.81), channel_id=1, replica_groups=mesh['groups'=2,'seq'=16,'heads'=8,'sub'=2] {'heads'}, dimensions={0} | all-to-all | bytes 8192 | tf_op jit(solution)/shard_map/all_to_all | solution.py:38
  502.4 0.0 copy-done.6
  502.4 0.8 fusion.22
  503.2 0.0 copy-done.2
  (46 shorter events, 0.7 us)
Async XLA Ops:
  9.1 3.2 copy-start
  24.2 46.4 %copy-start.4 = (bf16[128,128]{1,0:T(8,128)(2,1)S(1)}, bf16[128,128]{1,0:T(8,128)(2,1)}, u32[]{:S(2)}) copy-start(bf16[128,128]{1,0:T(8,128)(2,1)} %param.12) | copy-start | bytes 98308
  24.2 46.4 %copy-start.5 = (bf16[128,128]{1,0:T(8,128)(2,1)S(1)}, bf16[128,128]{1,0:T(8,128)(2,1)}, u32[]{:S(2)}) copy-start(bf16[128,128]{1,0:T(8,128)(2,1)} %param.11) | copy-start | bytes 98308
  24.2 47.1 %copy-start.7 = (s32[32]{0:T(128)S(1)}, s32[32]{0:T(128)}, u32[]{:S(2)}) copy-start(s32[32]{0:T(128)} %param.14) | copy-start | bytes 388
  24.2 47.4 %copy-start.8 = (s32[64]{0:T(128)S(1)}, s32[64]{0:T(128)}, u32[]{:S(2)}) copy-start(s32[64]{0:T(128)} %param.13) | copy-start | bytes 772
  24.2 160.1 %copy-start.10 = (bf16[128,1024]{1,0:T(8,128)(2,1)S(1)}, bf16[128,1024]{1,0:T(8,128)(2,1)}, u32[]{:S(2)}) copy-start(bf16[128,1024]{1,0:T(8,128)(2,1)} %param.10) | copy-start | bytes 786436
  24.3 416.9 %all-to-all-start = ((bf16[1024,32,128]{2,0,1:T(8,128)(2,1)}), bf16[1024,32,128]{2,0,1:T(8,128)(2,1)}, u32[]{:S(2)}, u32[]{:S(2)}) async-start(bf16[1024,32,128]{2,0,1:T(8,128)(2,1)} %copy.139), calls=%async_computation | async-start | bytes 16777216 | tf_op jit(solution)/shard_map/all_to_all | solution.py:12
  70.6 113.8 %all-gather.2.cloned.1.call-start = ((), (), s32[]{:S(2)}) async-start(), calls=%async_computation.3 | async-start | bytes 2162688 | tf_op jit(solution)/shard_map/all_gather | solution.py:21
  186.2 4.0 copy-start.9
  199.3 253.8 %copy-start.1 = (bf16[16,8,8,128]{3,1,2,0:T(8,128)(2,1)}, bf16[16,8,8,128]{3,1,2,0:T(8,128)(2,1)S(1)}, u32[]{:S(2)}) copy-start(bf16[16,8,8,128]{3,1,2,0:T(8,128)(2,1)S(1)} %copy.156) | copy-start | bytes 786436
  453.1 40.2 %copy-start.3 = (bf16[128,512]{1,0:T(8,128)(2,1)S(1)}, bf16[128,512]{1,0:T(8,128)(2,1)}, u32[]{:S(2)}) copy-start(bf16[128,512]{1,0:T(8,128)(2,1)} %param.16) | copy-start | bytes 393220
  453.1 49.4 %copy-start.6 = (f32[512]{0:T(512)S(1)}, f32[512]{0:T(512)}, u32[]{:S(2)}) copy-start(f32[512]{0:T(512)} %param.17) | copy-start | bytes 6148
  493.4 9.8 %copy-start.2 = (bf16[128,512]{1,0:T(8,128)(2,1)}, bf16[128,512]{1,0:T(8,128)(2,1)S(1)}, u32[]{:S(2)}) copy-start(bf16[128,512]{1,0:T(8,128)(2,1)S(1)} %get-tuple-element.26) | copy-start | bytes 393220
Sparse Core Ops, SparseCore 0:
  74.1 110.2 all-gather.1
